TPU v7x, 128 devices: a whole 4x4x4 slice. The times are simulated.
128 devices in a mesh: dp: 8 (over z, core), mp: 16 (over y, x).
Axes of the slice: x: 4, y: 4, z: 4, core: 2. Of those that a mesh axis runs over, the one named last changes fastest.
Arguments:
- patches: bfloat16 [16384, 1280], P(('dp', 'mp')), may hold values from -6 to 6
- window_ids: int32 [128, 128], P(('dp', 'mp')), may hold values from 0 to 7, never falling along the last dimension, each value on 1 to 64 neighbouring positions
- owner: int32 [4096, 1], P(('dp', 'mp')), may hold values from 0 to 7; in each aligned block of 32 rows (0 to 31, 32 to 63, ...) at most 8 rows name the same one
- slot_of_row: int32 [128, 64], P(('dp', 'mp')), may hold values from 0 to 63, each once within a row
- text_embeds: bfloat16 [8192, 8192], P(('dp', 'mp')), may hold values from -6 to 6
- vit_norm: float32 [1280], replicated, may hold values from 0.3 to 3
- vit_qkv_w: bfloat16 [1280, 1920], replicated, may hold values from -0.15625 to 0.15625
- vit_qkv_b: float32 [1920], replicated, may hold values from -12 to 12
- vit_out_w: bfloat16 [640, 1280], replicated, may hold values from -0.25 to 0.25
- merge_norm: float32 [1280], replicated, may hold values from 0.3 to 3
- merge_w1: bfloat16 [5120, 5120], P(None, 'mp'), may hold values from -0.078125 to 0.078125
- merge_b1: float32 [5120], P('mp'), may hold values from -3 to 3
- merge_w2: bfloat16 [5120, 8192], P('mp'), may hold values from -0.078125 to 0.078125
- merge_b2: float32 [8192], replicated, may hold values from -3 to 3
- llm_norm: float32 [8192], replicated, may hold values from 0.5 to 1.5
- q_w: bfloat16 [8192, 4096], P(None, 'mp'), may hold values from -0.0625 to 0.0625
- q_b: float32 [4096], P('mp'), may hold values from -12 to 12
- kv_w: bfloat16 [2, 8192, 512], P(None, None, 'mp'), may hold values from -0.0625 to 0.0625
- kv_b: float32 [2, 512], P(None, 'mp'), may hold values from -12 to 12
Outputs:
- attended: bfloat16 [8192, 4096], P('dp', 'mp')
Inputs may be any that keep to these rules, and one draw needn't show every extreme that they name: `window_ids`: within each block, window numbers never fall and each window has at most 64 patches. Among the 32 merged rows of one device, no owner is named by more than 8 rows, a bound that some block reaches. `slot_of_row`: each row is a permutation of the 64 slots.
All inputs are finite; a program needn't handle non-finite values.
Results may differ from a plain program's by a relative error of at most 0.04.
Values may be sent and summed in bfloat16 or wider, within the bound.
No kernel may reach another device: no remote copies, remote signals or barrier semaphores. Data moves between devices by JAX's collectives and lax.ppermute only.
A program may use at most 128 MiB of HBM per device.

v0:
```python
import jax
import jax.numpy as jnp
from jax import lax
from jax.sharding import PartitionSpec as P

VHD = 80
HD = 128
QH = 32
KVH = 4


epsilon = 1e-06


def laid_out(parts, dim):
    lengths = list(parts.shape[1:])
    lengths[dim] *= parts.shape[0]
    return jnp.moveaxis(parts, 0, dim).reshape(lengths)


def copy_for_each(x, axis):
    size = lax.axis_size(axis)
    return lax.all_to_all(jnp.broadcast_to(x[None], (size, *x.shape)), axis, 0, 0, tiled=True)


def gathered_copies(x, axis, dim):
    return laid_out(copy_for_each(x, axis), dim)


def rms_norm(inputs, gain):
    inputs = inputs.astype(jnp.float32)
    return inputs * lax.rsqrt(jnp.mean(inputs * inputs, axis=-1, keepdims=True) + epsilon) * gain


def vision_block(patches, window_ids, vit_norm, vit_qkv_w, vit_qkv_b, vit_out_w, merge_norm):
    normed = rms_norm(patches, vit_norm).astype(jnp.bfloat16)
    projected = (jnp.dot(normed, vit_qkv_w, preferred_element_type=jnp.float32) + vit_qkv_b).astype(
        jnp.bfloat16
    )
    blocks = window_ids.shape[0]
    width = window_ids.shape[1]
    inner_width = vit_out_w.shape[0]
    heads = inner_width // VHD
    shaped = projected.reshape(blocks, width, 3, heads, VHD)
    scores = jnp.einsum(
        "bqhd,bkhd->bhqk", shaped[:, :, 0], shaped[:, :, 1], preferred_element_type=jnp.float32
    ) * VHD ** (-0.5)
    in_window = window_ids[:, None, :, None] == window_ids[:, None, None, :]
    scores = jnp.where(in_window, scores, -1e30)
    peak = jnp.max(scores, axis=-1, keepdims=True)
    weights = jnp.exp(scores - peak)
    weights = (weights / jnp.sum(weights, axis=-1, keepdims=True)).astype(jnp.bfloat16)
    mixture = jnp.einsum(
        "bhqk,bkhd->bqhd", weights, shaped[:, :, 2], preferred_element_type=jnp.float32
    )
    mixture = mixture.astype(jnp.bfloat16).reshape(blocks * width, inner_width)
    residual = (
        patches.astype(jnp.float32)
        + jnp.dot(mixture, vit_out_w, preferred_element_type=jnp.float32)
    ).astype(jnp.bfloat16)
    merged = rms_norm(residual, merge_norm).astype(jnp.bfloat16)
    return merged.reshape(blocks * width // 4, 4 * patches.shape[1])


def shards(
    patches,
    window_ids,
    owner,
    slot_of_row,
    text_embeds,
    vit_norm,
    vit_qkv_w,
    vit_qkv_b,
    vit_out_w,
    merge_norm,
    merge_w1,
    merge_b1,
    merge_w2,
    merge_b2,
    llm_norm,
    q_w,
    q_b,
    kv_w,
    kv_b,
):
    merged = vision_block(
        patches, window_ids, vit_norm, vit_qkv_w, vit_qkv_b, vit_out_w, merge_norm
    )
    own_index = lax.axis_index("mp")
    rows_all = lax.all_gather(merged, "mp", axis=0, tiled=True)
    hidden = jax.nn.gelu(
        jnp.dot(rows_all, merge_w1, preferred_element_type=jnp.float32) + merge_b1,
        approximate=False,
    ).astype(jnp.bfloat16)
    own_rows = lax.psum_scatter(
        jnp.dot(hidden, merge_w2, preferred_element_type=jnp.float32).astype(jnp.bfloat16),
        "mp",
        scatter_dimension=0,
        tiled=True,
    ).astype(jnp.float32)
    embedded = (own_rows + merge_b2).astype(jnp.bfloat16)
    seq_rows = text_embeds.shape[0]
    groups = lax.axis_size("dp")
    capacity = seq_rows // groups
    target_group = owner[:, 0]
    onehot = (target_group[:, None] == jnp.arange(groups, dtype=jnp.int32)[None, :]).astype(
        jnp.int32
    )
    rank_in = jnp.sum((jnp.cumsum(onehot, axis=0) - onehot) * onehot, axis=1)
    send_slot = target_group * capacity + rank_in
    selector = send_slot[None, :] == jnp.arange(seq_rows, dtype=jnp.int32)[:, None]
    buffer = jnp.dot(
        selector.astype(jnp.bfloat16), embedded, preferred_element_type=jnp.float32
    ).astype(jnp.bfloat16)
    buffer = buffer.reshape(groups, capacity, embedded.shape[1])
    marks = jnp.sum(selector.astype(jnp.int32), axis=1).reshape(groups, capacity)
    arrived, arrived_marks = (
        lax.all_to_all(buffer, "dp", split_axis=0, concat_axis=0, tiled=True),
        lax.all_to_all(marks, "dp", split_axis=0, concat_axis=0, tiled=True),
    )
    arrived = arrived.reshape(seq_rows, embedded.shape[1])
    arrived_marks = arrived_marks.reshape(seq_rows)
    chosen = slot_of_row[0]
    sequence = jnp.where(arrived_marks[chosen][:, None] > 0, arrived[chosen], text_embeds)
    llm_normed = rms_norm(sequence, llm_norm).astype(jnp.bfloat16)
    query_cols = q_w.shape[1]
    kv_cols = kv_w.shape[2]
    shard_rows = lax.all_gather(llm_normed, "mp", axis=0, tiled=True)
    projected = jnp.concatenate(
        [
            jnp.dot(shard_rows, q_w, preferred_element_type=jnp.float32),
            jnp.dot(shard_rows, kv_w[0], preferred_element_type=jnp.float32),
            jnp.dot(shard_rows, kv_w[1], preferred_element_type=jnp.float32),
        ],
        axis=1,
    )
    length = projected.shape[0]
    queries = (projected[:, :query_cols] + q_b).astype(jnp.bfloat16)
    key_rows = (projected[:, query_cols : query_cols + kv_cols] + kv_b[0]).astype(jnp.bfloat16)
    value_rows = (projected[:, query_cols + kv_cols :] + kv_b[1]).astype(jnp.bfloat16)
    stacked = jnp.stack([key_rows.T, value_rows.T])
    all_heads = gathered_copies(stacked, "mp", 1)
    heads_here = query_cols // HD
    group_size = QH // KVH
    kv_head = own_index * heads_here // group_size
    by_head = all_heads.reshape(2, HD, KVH, length)
    key_cols = lax.dynamic_index_in_dim(by_head[0], kv_head, 1, keepdims=False)
    value_cols = lax.dynamic_index_in_dim(by_head[1], kv_head, 1, keepdims=False)
    query_heads = queries.reshape(length, heads_here, HD)
    scores = jnp.einsum(
        "qhd,dk->hqk", query_heads, key_cols, preferred_element_type=jnp.float32
    ) * HD ** (-0.5)
    allowed = jnp.arange(length)[:, None] >= jnp.arange(length)[None, :]
    scores = jnp.where(allowed[None], scores, -1e30)
    peak = jnp.max(scores, axis=-1, keepdims=True)
    weights = jnp.exp(scores - peak)
    weights = (weights / jnp.sum(weights, axis=-1, keepdims=True)).astype(jnp.bfloat16)
    mixture = jnp.einsum("hqk,dk->qhd", weights, value_cols, preferred_element_type=jnp.float32)
    return mixture.astype(jnp.bfloat16).reshape(length, query_cols)


def solution(mesh):
    return jax.shard_map(
        shards,
        mesh=mesh,
        in_specs=(
            P(("dp", "mp"), None),
            P(("dp", "mp"), None),
            P(("dp", "mp"), None),
            P(("dp", "mp"), None),
            P(("dp", "mp"), None),
            P(),
            P(),
            P(),
            P(),
            P(),
            P(None, "mp"),
            P("mp"),
            P("mp", None),
            P(),
            P(),
            P(None, "mp"),
            P("mp"),
            P(None, None, "mp"),
            P(None, "mp"),
        ),
        out_specs=P("dp", "mp"),
        check_vma=False,
    )
```

profile of v0, /device:TPU:0, one launch (start us, length us, event | category | flops | bytes accessed | tf_op | source)
XLA Modules:
  0.0 402.4 jit_solution(15220331925522827266)
XLA Ops:
  6.5 0.9 broadcast_compare_fusion
  7.5 1.2 fusion.25
  8.7 4.3 %fusion.10 = bf16[128,1920]{1,0:T(8,128)(2,1)} fusion(bf16[1280,1920]{1,0:T(8,128)(2,1)} %param.25, f32[1920]{0:T(1024)} %param.26, bf16[128,1280]{1,0:T(8,128)(2,1)} %param.19, f32[1280]{0:T(1024)} %param.24, f32[128]{0:T(128)S(1)} %add_rsqrt_fusion.2), kind=kOutput, calls=%fused_computation.22 | convolution fusion | flops 630292480 | bytes 5747712 | tf_op jit(solution)/shard_map/dot_general | solution.py:37
  12.9 2.0 copy.47
  15.0 1.4 fusion.119
  16.3 2.1 fusion.18
  18.4 1.5 convolution_convert_fusion.2
  19.9 2.0 multiply_reduce_fusion
  22.8 1.9 reshape.196
  24.8 58.6 %all-gather.3.cloned.1.call-done = bf16[512,5120]{1,0:T(8,128)(2,1)} async-done(((bf16[32,5120]{1,0:T(8,128)(2,1)}), bf16[512,5120]{1,0:T(8,128)(2,1)}) %all-gather.3.cloned.1.call-update) | async-done | bytes 5242896 | tf_op jit(solution)/shard_map/all_gather | solution.py:90
  83.4 16.7 %convolution_convert_fusion = bf16[512,8192]{1,0:T(8,128)(2,1)} fusion(bf16[320,8192]{1,0:T(8,128)(2,1)} %param.31, bf16[512,5120]{1,0:T(8,128)(2,1)} %all-gather.3.cloned.1.call-done, bf16[5120,320]{0,1:T(8,128)(2,1)S(1)} %copy-done, f32[320]{0:T(512)S(1)} %copy-done.10), kind=kOutput, calls=%fused_computation.4 | convolution fusion | flops 4377083904 | bytes 22152448 | tf_op jit(solution)/shard_map/dot_general | solution.py:96
  101.8 4.4 %all-to-all-start = ((s32[8,1,8]{2,1,0:T(1,128)}), s32[8,1,8]{2,1,0:T(1,128)S(1)}, u32[]{:S(2)}, u32[]{:S(2)}) async-start(s32[8,1,8]{2,1,0:T(1,128)} %bitcast.1), calls=%async_computation | async-start | bytes 8192 | tf_op jit(solution)/shard_map/all_to_all | solution.py:119
  106.2 79.8 %reduce-scatter.2.cloned.1.call-done = bf16[32,8192]{1,0:T(8,128)(2,1)} async-done(((bf16[512,8192]{1,0:T(8,128)(2,1)}), bf16[32,8192]{1,0:T(8,128)(2,1)}) %reduce-scatter.2.cloned.1.call-update) | async-done | bytes 524304 | tf_op jit(solution)/shard_map/reduce_scatter | solution.py:95
  186.0 2.6 fusion.2
  188.6 4.4 %all-to-all-start.1 = ((bf16[8,8,8192]{2,1,0:T(8,128)(2,1)}), bf16[8,8,8192]{2,1,0:T(8,128)(2,1)S(1)}, u32[]{:S(2)}, u32[]{:S(2)}) async-start(bf16[8,8,8192]{2,1,0:T(8,128)(2,1)} %fusion.2), calls=%async_computation.2 | async-start | bytes 2097152 | tf_op jit(solution)/shard_map/all_to_all | solution.py:118
  195.4 13.6 %all-to-all-done.1 = bf16[8,8,8192]{2,1,0:T(8,128)(2,1)S(1)} async-done(((bf16[8,8,8192]{2,1,0:T(8,128)(2,1)}), bf16[8,8,8192]{2,1,0:T(8,128)(2,1)S(1)}, u32[]{:S(2)}, u32[]{:S(2)}) %all-to-all-start.1) | async-done | bytes 1048608 | tf_op jit(solution)/shard_map/all_to_all | solution.py:118
  209.0 1.2 gather_fusion.1
  210.8 1.5 fusion.13
  212.3 108.6 %all-gather.5.cloned.1.call-done = bf16[1024,8192]{1,0:T(8,128)(2,1)} async-done(((bf16[64,8192]{1,0:T(8,128)(2,1)}), bf16[1024,8192]{1,0:T(8,128)(2,1)}) %all-gather.5.cloned.1.call-update) | async-done | bytes 16777232 | tf_op jit(solution)/shard_map/all_gather | solution.py:128
  320.9 10.9 %fusion.21 = bf16[1,32,1024]{2,1,0:T(8,128)(2,1)S(1)} fusion(bf16[1024,8192]{1,0:T(8,128)(2,1)} %all-gather.5.cloned.1.call-done, bf16[2,8192,32]{1,2,0:T(8,128)(2,1)S(1)} %copy-done.4, f32[32]{0:T(128)S(1)} %get-tuple-element.8), kind=kOutput, calls=%fused_computation.39 | convolution fusion | flops 536936448 | bytes 17367552 | tf_op jit(solution)/shard_map/dot_general | solution.py:133
  331.8 5.0 %fusion.22 = bf16[1,32,1024]{2,1,0:T(8,128)(2,1)S(1)} fusion(bf16[1024,8192]{1,0:T(8,128)(2,1)S(1)} %copy-done.2, bf16[2,8192,32]{1,2,0:T(8,128)(2,1)S(1)} %copy-done.4, f32[32]{0:T(128)S(1)} %get-tuple-element.7), kind=kOutput, calls=%fused_computation.40 | convolution fusion | flops 536936448 | bytes 17367552 | tf_op jit(solution)/shard_map/dot_general | solution.py:132
  336.9 1.6 broadcast_in_dim.33
  338.5 5.3 %all-to-all-start.2 = ((bf16[16,2,32,1024]{3,2,1,0:T(8,128)(2,1)}), bf16[16,2,32,1024]{3,2,1,0:T(8,128)(2,1)S(1)}, u32[]{:S(2)}, u32[]{:S(2)}) async-start(bf16[16,2,32,1024]{3,2,1,0:T(8,128)(2,1)} %broadcast_in_dim.33), calls=%async_computation.3 | async-start | bytes 4194304 | tf_op jit(solution)/shard_map/all_to_all | solution.py:23
  343.8 1.3 iota_compare_fusion
  345.1 10.0 %fusion.14 = bf16[1024,256]{0,1:T(8,128)(2,1)} fusion(bf16[1024,8192]{1,0:T(8,128)(2,1)} %all-gather.5.cloned.1.call-done, bf16[8192,256]{1,0:T(8,128)(2,1)} %param.34, f32[256]{0:T(256)S(1)} %copy-done.11), kind=kOutput, calls=%fused_computation.27 | convolution fusion | flops 4295491584 | bytes 21496832 | tf_op jit(solution)/shard_map/dot_general | solution.py:131
  355.2 20.0 %all-to-all-done.2 = bf16[16,2,32,1024]{3,2,1,0:T(8,128)(2,1)S(1)} async-done(((bf16[16,2,32,1024]{3,2,1,0:T(8,128)(2,1)}), bf16[16,2,32,1024]{3,2,1,0:T(8,128)(2,1)S(1)}, u32[]{:S(2)}, u32[]{:S(2)}) %all-to-all-start.2) | async-done | bytes 2097184 | tf_op jit(solution)/shard_map/all_to_all | solution.py:23
  375.2 1.3 fusion.118
  376.4 1.5 squeeze.34
  378.3 1.9 constant_dynamic-slice_fusion
  380.7 7.8 %fusion.120 = (f32[2,1024]{1,0:T(2,128)S(1)}, f32[2,1024,1024]{1,2,0:T(8,128)}) fusion(pred[1024,1024]{0,1:T(8,128)(4,1)} %iota_compare_fusion, bf16[1024,2,128]{0,2,1:T(8,128)(2,1)} %bitcast.116, bf16[128,1,1024]{0,2,1:T(8,128)(2,1)S(1)} %copy.49), kind=kOutput, calls=%fused_computation.168 | convolution fusion | flops 545260544 | bytes 10231808 | tf_op jit(solution)/shard_map/sub | solution.py:156
  388.5 5.3 %fusion.15 = bf16[128,2,1024]{2,0,1:T(8,128)(2,1)} fusion(f32[2,1024,1024]{1,2,0:T(8,128)} %get-tuple-element.12, f32[2,1024]{1,0:T(2,128)S(1)} %get-tuple-element.11, bf16[128,1,1024]{2,1,0:T(2,128)(2,1)} %get-tuple-element.14), kind=kOutput, calls=%fused_computation.28 | convolution fusion | flops 541327360 | bytes 9183232 | tf_op jit(solution)/shard_map/hqk,dk->qhd/dot_general | solution.py:158
  393.8 2.0 copy.52
  (55 shorter events, 6.4 us)
Async XLA Ops:
  6.5 76.9 %copy-start = (bf16[5120,320]{0,1:T(8,128)(2,1)S(1)}, bf16[5120,320]{0,1:T(8,128)(2,1)}, u32[]{:S(2)}) copy-start(bf16[5120,320]{0,1:T(8,128)(2,1)} %param.29) | copy-start | bytes 9830404
  6.5 76.9 %all-gather.3.cloned.1.call-start = ((), (), s32[]{:S(2)}) async-start(), calls=%async_computation.4 | async-start | bytes 5570560 | tf_op jit(solution)/shard_map/all_gather | solution.py:90
  12.9 9.0 %copy-start.7 = (f32[1280]{0:T(1024)S(1)}, f32[1280]{0:T(1024)}, u32[]{:S(2)}) copy-start(f32[1280]{0:T(1024)} %param.28) | copy-start | bytes 15364
  12.9 70.5 %copy-start.10 = (f32[320]{0:T(512)S(1)}, f32[320]{0:T(512)}, u32[]{:S(2)}) copy-start(f32[320]{0:T(512)} %param.30) | copy-start | bytes 3844
  24.7 161.3 %reduce-scatter.2.cloned.1.call-start = ((), (), s32[]{:S(2)}) async-start(), calls=%async_computation.5 | async-start | bytes 8912896 | tf_op jit(solution)/shard_map/reduce_scatter | solution.py:95
  100.1 0.7 copy-start.8
  100.1 86.0 %copy-start.6 = (f32[8192]{0:T(1024)S(1)}, f32[8192]{0:T(1024)}, u32[]{:S(2)}) copy-start(f32[8192]{0:T(1024)} %param.32) | copy-start | bytes 98308
  100.1 93.2 %copy-start.12 = (s32[1,64]{1,0:T(1,128)S(1)}, s32[1,64]{1,0:T(1,128)}, u32[]{:S(2)}) copy-start(s32[1,64]{1,0:T(1,128)} %param.22) | copy-start | bytes 772
  101.8 86.8 %all-to-all-start = ((s32[8,1,8]{2,1,0:T(1,128)}), s32[8,1,8]{2,1,0:T(1,128)S(1)}, u32[]{:S(2)}, u32[]{:S(2)}) async-start(s32[8,1,8]{2,1,0:T(1,128)} %bitcast.1), calls=%async_computation | async-start | bytes 8192 | tf_op jit(solution)/shard_map/all_to_all | solution.py:119
  188.6 20.4 %all-to-all-start.1 = ((bf16[8,8,8192]{2,1,0:T(8,128)(2,1)}), bf16[8,8,8192]{2,1,0:T(8,128)(2,1)S(1)}, u32[]{:S(2)}, u32[]{:S(2)}) async-start(bf16[8,8,8192]{2,1,0:T(8,128)(2,1)} %fusion.2), calls=%async_computation.2 | async-start | bytes 2097152 | tf_op jit(solution)/shard_map/all_to_all | solution.py:118
  193.0 17.1 %copy-start.3 = (bf16[64,8192]{1,0:T(8,128)(2,1)S(1)}, bf16[64,8192]{1,0:T(8,128)(2,1)}, u32[]{:S(2)}) copy-start(bf16[64,8192]{1,0:T(8,128)(2,1)} %param.23) | copy-start | bytes 3145732
  193.0 127.8 %all-gather.5.cloned.1.call-start = ((), (), s32[]{:S(2)}) async-start(), calls=%async_computation.6 | async-start | bytes 17825792 | tf_op jit(solution)/shard_map/all_gather | solution.py:128
  209.0 1.8 copy-start.5
  210.2 2.1 copy-start.9
  210.2 110.7 %copy-start.4 = (bf16[2,8192,32]{1,2,0:T(8,128)(2,1)S(1)}, bf16[2,8192,32]{1,2,0:T(8,128)(2,1)}, u32[]{:S(2)}) copy-start(bf16[2,8192,32]{1,2,0:T(8,128)(2,1)} %param.36) | copy-start | bytes 3145732
  320.9 11.0 %copy-start.2 = (bf16[1024,8192]{1,0:T(8,128)(2,1)S(1)}, bf16[1024,8192]{1,0:T(8,128)(2,1)}, u32[]{:S(2)}) copy-start(bf16[1024,8192]{1,0:T(8,128)(2,1)} %all-gather.5.cloned.1.call-done) | copy-start | bytes 50331652
  336.9 8.2 %copy-start.11 = (f32[256]{0:T(256)S(1)}, f32[256]{0:T(256)}, u32[]{:S(2)}) copy-start(f32[256]{0:T(256)} %param.35) | copy-start | bytes 3076
  338.5 36.6 %all-to-all-start.2 = ((bf16[16,2,32,1024]{3,2,1,0:T(8,128)(2,1)}), bf16[16,2,32,1024]{3,2,1,0:T(8,128)(2,1)S(1)}, u32[]{:S(2)}, u32[]{:S(2)}) async-start(bf16[16,2,32,1024]{3,2,1,0:T(8,128)(2,1)} %broadcast_in_dim.33), calls=%async_computation.3 | async-start | bytes 4194304 | tf_op jit(solution)/shard_map/all_to_all | solution.py:23
  388.5 7.4 %copy-start.1 = (bf16[5120,320]{0,1:T(8,128)(2,1)S(1)}, bf16[5120,320]{0,1:T(8,128)(2,1)}, u32[]{:S(2)}) copy-start(bf16[5120,320]{0,1:T(8,128)(2,1)} %param.29) | copy-start | bytes 9830404
Sparse Core Ops, SparseCore 0:
  24.8 58.5 all-gather.2
  100.2 85.7 reduce-scatter.1
  212.4 108.4 all-gather.4
where the time goes:
time: 403 us; the launch traced here: 402 us
  waiting for transfers between devices  281 us (70%)
  matrix products  69.6 us (17%)
  local copies, waits for them, and re-layouts  17 us (4%)
  starting transfers between devices  14.4 us (4%)
  between operations  13.3 us (3%)
  other arithmetic  7.39 us (2%)
    all_gather x1, waiting for transfers between devices, shards(): shard_rows = lax.all_gather(llm_normed, 'mp', axis=0, tiled=True)  109 us
    reduce_scatter x1, waiting for transfers between devices, shards(): lax.psum_scatter(jnp.dot(hidden, merge_w2, preferred_element_type=jnp.flo...  79.8 us
    all_gather x1, waiting for transfers between devices, shards(): rows_all = lax.all_gather(merged, 'mp', axis=0, tiled=True)  58.6 us
    all_to_all x1, waiting for transfers between devices, copy_for_each(): lax.all_to_all(jnp.broadcast_to(x[None], (size, *x.shape)), axis, 0, 0, t...  20 us
    dot_general x1, matrix products, shards(): jnp.dot(hidden, merge_w2, preferred_element_type=jnp.float32)  16.7 us
    all_to_all x1, waiting for transfers between devices, shards(): lax.all_to_all(buffer, 'dp', split_axis=0, concat_axis=0, tiled=True)  13.6 us
    dot_general x1, matrix products, shards(): jnp.dot(shard_rows, kv_w[1], preferred_element_type=jnp.float32)  10.9 us
    dot_general x1, matrix products, shards(): jnp.dot(shard_rows, q_w, preferred_element_type=jnp.float32)  10 us
  transfers between devices with their start and end apart: 6, of which 5 were waited for; matrix products, arithmetic and copies ran while one was open for 4% of the time, Pallas kernels for 0%

commit v1 on v0

--- a/solution.py
+++ b/solution.py
@@ -1,30 +1,16 @@
 import jax
 import jax.numpy as jnp
 from jax import lax
+from jax.experimental import pallas as pl
+from jax.experimental.pallas import tpu as pltpu
 from jax.sharding import PartitionSpec as P
 
 VHD = 80
 HD = 128
-QH = 32
 KVH = 4
 
 
 epsilon = 1e-06
-
-
-def laid_out(parts, dim):
-    lengths = list(parts.shape[1:])
-    lengths[dim] *= parts.shape[0]
-    return jnp.moveaxis(parts, 0, dim).reshape(lengths)
-
-
-def copy_for_each(x, axis):
-    size = lax.axis_size(axis)
-    return lax.all_to_all(jnp.broadcast_to(x[None], (size, *x.shape)), axis, 0, 0, tiled=True)
-
-
-def gathered_copies(x, axis, dim):
-    return laid_out(copy_for_each(x, axis), dim)
 
 
 def rms_norm(inputs, gain):
@@ -86,7 +72,6 @@
     merged = vision_block(
         patches, window_ids, vit_norm, vit_qkv_w, vit_qkv_b, vit_out_w, merge_norm
     )
-    own_index = lax.axis_index("mp")
     rows_all = lax.all_gather(merged, "mp", axis=0, tiled=True)
     hidden = jax.nn.gelu(
         jnp.dot(rows_all, merge_w1, preferred_element_type=jnp.float32) + merge_b1,
@@ -123,40 +108,72 @@
     chosen = slot_of_row[0]
     sequence = jnp.where(arrived_marks[chosen][:, None] > 0, arrived[chosen], text_embeds)
     llm_normed = rms_norm(sequence, llm_norm).astype(jnp.bfloat16)
-    query_cols = q_w.shape[1]
     kv_cols = kv_w.shape[2]
     shard_rows = lax.all_gather(llm_normed, "mp", axis=0, tiled=True)
-    projected = jnp.concatenate(
-        [
-            jnp.dot(shard_rows, q_w, preferred_element_type=jnp.float32),
-            jnp.dot(shard_rows, kv_w[0], preferred_element_type=jnp.float32),
-            jnp.dot(shard_rows, kv_w[1], preferred_element_type=jnp.float32),
-        ],
-        axis=1,
-    )
-    length = projected.shape[0]
-    queries = (projected[:, :query_cols] + q_b).astype(jnp.bfloat16)
-    key_rows = (projected[:, query_cols : query_cols + kv_cols] + kv_b[0]).astype(jnp.bfloat16)
-    value_rows = (projected[:, query_cols + kv_cols :] + kv_b[1]).astype(jnp.bfloat16)
-    stacked = jnp.stack([key_rows.T, value_rows.T])
-    all_heads = gathered_copies(stacked, "mp", 1)
-    heads_here = query_cols // HD
-    group_size = QH // KVH
-    kv_head = own_index * heads_here // group_size
-    by_head = all_heads.reshape(2, HD, KVH, length)
-    key_cols = lax.dynamic_index_in_dim(by_head[0], kv_head, 1, keepdims=False)
-    value_cols = lax.dynamic_index_in_dim(by_head[1], kv_head, 1, keepdims=False)
-    query_heads = queries.reshape(length, heads_here, HD)
-    scores = jnp.einsum(
-        "qhd,dk->hqk", query_heads, key_cols, preferred_element_type=jnp.float32
-    ) * HD ** (-0.5)
-    allowed = jnp.arange(length)[:, None] >= jnp.arange(length)[None, :]
-    scores = jnp.where(allowed[None], scores, -1e30)
-    peak = jnp.max(scores, axis=-1, keepdims=True)
-    weights = jnp.exp(scores - peak)
-    weights = (weights / jnp.sum(weights, axis=-1, keepdims=True)).astype(jnp.bfloat16)
-    mixture = jnp.einsum("hqk,dk->qhd", weights, value_cols, preferred_element_type=jnp.float32)
-    return mixture.astype(jnp.bfloat16).reshape(length, query_cols)
+    queries = (jnp.dot(shard_rows, q_w, preferred_element_type=jnp.float32) + q_b).astype(
+        jnp.bfloat16
+    )
+    length = shard_rows.shape[0]
+    kv_rows = lax.dot_general(
+        kv_w, shard_rows, (((1,), (1,)), ((), ())), preferred_element_type=jnp.float32
+    )
+    kv_rows = (kv_rows + kv_b[:, :, None]).astype(jnp.bfloat16)
+    shards_mp = lax.axis_size("mp")
+    dims_here = kv_cols // KVH
+    by_head = jnp.swapaxes(kv_rows.reshape(2, dims_here, KVH, length), 1, 2)
+    for_each = jnp.broadcast_to(
+        by_head[:, :, None], (2, KVH, shards_mp // KVH, dims_here, length)
+    ).reshape(2, shards_mp, dims_here, length)
+    own_head = lax.all_to_all(for_each, "mp", 1, 1, tiled=True).reshape(2, HD, length)
+    return attention(queries, own_head[0], own_head[1])
+
+
+def attention_kernel(queries_ref, keys_ref, values_ref, out_ref):
+    length, cols = queries_ref.shape
+    block = 256
+    scale = HD ** (-0.5)
+    row = lax.broadcasted_iota(jnp.int32, (block, block), 0)
+    col = lax.broadcasted_iota(jnp.int32, (block, block), 1)
+    allowed = row >= col
+    for head in range(cols // HD):
+        lanes = slice(head * HD, (head + 1) * HD)
+        for first in range(0, length, block):
+            last = first + block
+            own = queries_ref[first:last, lanes]
+            diagonal = jnp.dot(
+                own, keys_ref[:, first:last], preferred_element_type=jnp.float32
+            )
+            diagonal = jnp.where(allowed, diagonal, -1e30)
+            peak = jnp.max(diagonal, axis=-1, keepdims=True)
+            if first:
+                before = jnp.dot(own, keys_ref[:, :first], preferred_element_type=jnp.float32)
+                peak = jnp.maximum(peak, jnp.max(before, axis=-1, keepdims=True))
+            weights = jnp.exp((diagonal - peak) * scale)
+            total = jnp.sum(weights, axis=-1, keepdims=True)
+            mixed = lax.dot_general(
+                weights.astype(jnp.bfloat16),
+                values_ref[:, first:last],
+                (((1,), (1,)), ((), ())),
+                preferred_element_type=jnp.float32,
+            )
+            if first:
+                weights = jnp.exp((before - peak) * scale)
+                total = total + jnp.sum(weights, axis=-1, keepdims=True)
+                mixed = mixed + lax.dot_general(
+                    weights.astype(jnp.bfloat16),
+                    values_ref[:, :first],
+                    (((1,), (1,)), ((), ())),
+                    preferred_element_type=jnp.float32,
+                )
+            out_ref[first:last, lanes] = (mixed / total).astype(jnp.bfloat16)
+
+
+def attention(queries, keys, values):
+    return pl.pallas_call(
+        attention_kernel,
+        out_shape=jax.ShapeDtypeStruct(queries.shape, jnp.bfloat16),
+        name="causal_attention",
+    )(queries, keys, values)
 
 
 def solution(mesh):

time: 403 us -> 371 us (0.921)
  waiting for transfers between devices: 281 us -> 261 us
  matrix products: 69.6 us -> 54 us
  Pallas kernels: 0 us -> 5.02 us
    all_to_all x1, waiting for transfers between devices: 20 us -> 0.01 us  [shards(): lax.all_to_all(for_each, 'mp', 1, 1, tiled=True).reshape(2, HD, length)]
    dot_general x4 -> x1, matrix products: 31.3 us -> 12.3 us  [shards(): jnp.dot(shard_rows, q_w, preferred_element_type=jnp.float32) + q_b]
    unnamed x0 -> x1, matrix products: none -> 11.2 us
    sub x1 -> x0, matrix products: 7.83 us -> none  [shards(): weights = jnp.exp(scores - peak)]
    pallas_call x0 -> x1, Pallas kernels: none -> 5.02 us  [attention(): pl.pallas_call(attention_kernel, out_shape=jax.ShapeDtypeStruct(queries.s...]
  transfers between devices with their start and end apart: 6 -> 6, of which waited for: 5 -> 4; matrix products, arithmetic and copies ran while one was open for 4% -> 5% of each run, Pallas kernels for 0% -> 0%
where the time goes in v1:
time: 371 us; the launch traced here: 370 us
  waiting for transfers between devices  261 us (70%)
  matrix products  54 us (15%)
  starting transfers between devices  14.5 us (4%)
  local copies, waits for them, and re-layouts  13.9 us (4%)
  between operations  13.2 us (4%)
  other arithmetic  9.17 us (2%)
  Pallas kernels  5.02 us (1%)
    all_gather x1, waiting for transfers between devices, shards(): shard_rows = lax.all_gather(llm_normed, 'mp', axis=0, tiled=True)  109 us
    reduce_scatter x1, waiting for transfers between devices, shards(): lax.psum_scatter(jnp.dot(hidden, merge_w2, preferred_element_type=jnp.flo...  79.6 us
    all_gather x1, waiting for transfers between devices, shards(): rows_all = lax.all_gather(merged, 'mp', axis=0, tiled=True)  58.6 us
    dot_general x1, matrix products, shards(): jnp.dot(hidden, merge_w2, preferred_element_type=jnp.float32)  16.7 us
    all_to_all x1, waiting for transfers between devices, shards(): lax.all_to_all(buffer, 'dp', split_axis=0, concat_axis=0, tiled=True)  13.7 us
    dot_general x1, matrix products, shards(): jnp.dot(shard_rows, q_w, preferred_element_type=jnp.float32) + q_b  12.3 us
    unnamed x1, matrix products  11.2 us
  transfers between devices with their start and end apart: 6, of which 4 were waited for; matrix products, arithmetic and copies ran while one was open for 5% of the time, Pallas kernels for 0%

profile of v1, /device:TPU:0, one launch (start us, length us, event | category | flops | bytes accessed | tf_op | source)
XLA Modules:
  0.0 370.5 jit_solution(1180798045535239328)
XLA Ops:
  6.5 1.3 fusion.12
  7.8 0.8 broadcast_compare_fusion
  8.6 4.3 %fusion.4 = bf16[128,1920]{1,0:T(8,128)(2,1)} fusion(bf16[1280,1920]{1,0:T(8,128)(2,1)} %param.25, f32[1920]{0:T(1024)} %param.26, bf16[128,1280]{1,0:T(8,128)(2,1)} %param.19, f32[1280]{0:T(1024)} %param.24, f32[128]{0:T(128)S(1)} %add_rsqrt_fusion.2), kind=kOutput, calls=%fused_computation.12 | convolution fusion | flops 630292480 | bytes 5747712 | tf_op jit(solution)/shard_map/dot_general | solution.py:23
  12.9 2.0 copy.33
  14.9 1.4 fusion.91
  16.3 2.1 fusion.11
  18.4 1.6 convolution_convert_fusion.2
  20.0 2.0 multiply_reduce_fusion
  22.0 0.8 multiply_convert_fusion
  22.9 1.9 reshape.184
  24.8 58.6 %all-gather.3.cloned.1.call-done = bf16[512,5120]{1,0:T(8,128)(2,1)} async-done(((bf16[32,5120]{1,0:T(8,128)(2,1)}), bf16[512,5120]{1,0:T(8,128)(2,1)}) %all-gather.3.cloned.1.call-update) | async-done | bytes 5242896 | tf_op jit(solution)/shard_map/all_gather | solution.py:75
  83.5 16.7 %convolution_convert_fusion = bf16[512,8192]{1,0:T(8,128)(2,1)} fusion(bf16[320,8192]{1,0:T(8,128)(2,1)} %param.31, bf16[512,5120]{1,0:T(8,128)(2,1)} %all-gather.3.cloned.1.call-done, bf16[5120,320]{0,1:T(8,128)(2,1)S(1)} %copy-done, f32[320]{0:T(512)S(1)} %copy-done.6), kind=kOutput, calls=%fused_computation.3 | convolution fusion | flops 4377083904 | bytes 22152448 | tf_op jit(solution)/shard_map/dot_general | solution.py:81
  100.2 0.6 copy-done.4
  101.2 0.7 all_to_all.12
  101.9 4.4 %all-to-all-start = ((s32[8,1,8]{2,1,0:T(1,128)}), s32[8,1,8]{2,1,0:T(1,128)S(1)}, u32[]{:S(2)}, u32[]{:S(2)}) async-start(s32[8,1,8]{2,1,0:T(1,128)} %bitcast.1), calls=%async_computation | async-start | bytes 8192 | tf_op jit(solution)/shard_map/all_to_all | solution.py:104
  106.3 79.6 %reduce-scatter.2.cloned.1.call-done = bf16[32,8192]{1,0:T(8,128)(2,1)} async-done(((bf16[512,8192]{1,0:T(8,128)(2,1)}), bf16[32,8192]{1,0:T(8,128)(2,1)}) %reduce-scatter.2.cloned.1.call-update) | async-done | bytes 524304 | tf_op jit(solution)/shard_map/reduce_scatter | solution.py:80
  185.9 2.6 fusion.1
  188.5 4.5 %all-to-all-start.1 = ((bf16[8,8,8192]{2,1,0:T(8,128)(2,1)}), bf16[8,8,8192]{2,1,0:T(8,128)(2,1)}, u32[]{:S(2)}, u32[]{:S(2)}) async-start(bf16[8,8,8192]{2,1,0:T(8,128)(2,1)} %fusion.1), calls=%async_computation.2 | async-start | bytes 2097152 | tf_op jit(solution)/shard_map/all_to_all | solution.py:103
  193.2 0.5 broadcast.147
  193.7 0.7 reduce.7
  194.5 0.8 gather_fusion
  195.3 13.7 %all-to-all-done.1 = bf16[8,8,8192]{2,1,0:T(8,128)(2,1)} async-done(((bf16[8,8,8192]{2,1,0:T(8,128)(2,1)}), bf16[8,8,8192]{2,1,0:T(8,128)(2,1)}, u32[]{:S(2)}, u32[]{:S(2)}) %all-to-all-start.1) | async-done | bytes 1048608 | tf_op jit(solution)/shard_map/all_to_all | solution.py:103
  209.0 4.5 %gather_fusion.1 = bf16[64,8192]{1,0:T(8,128)(2,1)} fusion(bf16[64,8192]{1,0:T(8,128)(2,1)} %bitcast.13, s32[1024]{0:T(1024)S(1)} %pad_clamp_fusion), kind=kCustom, calls=%fused_computation.1 | custom fusion | bytes 2097408 | tf_op jit(solution)/shard_map/gather | solution.py:109
  213.5 2.0 fusion.5
  215.6 3.0 fusion.7
  218.6 108.6 %all-gather.5.cloned.1.call-done = bf16[1024,8192]{1,0:T(8,128)(2,1)} async-done(((bf16[64,8192]{1,0:T(8,128)(2,1)}), bf16[1024,8192]{1,0:T(8,128)(2,1)}) %all-gather.5.cloned.1.call-update) | async-done | bytes 16777232 | tf_op jit(solution)/shard_map/all_gather | solution.py:112
  327.2 11.2 %fusion.92 = f32[1024,64]{0,1:S(1)} fusion(bf16[1024,8192]{1,0:T(8,128)(2,1)} %all-gather.5.cloned.1.call-done, bf16[8192,64]{0,1:T(8,128)(2,1)} %bitcast.62), kind=kOutput, calls=%fused_computation.137 | convolution fusion | flops 1073741824 | bytes 18087936
  338.6 0.9 broadcast_in_dim.22
  339.5 5.3 %all-to-all-start.2 = ((bf16[2,16,8,1024]{3,2,0,1:T(8,128)(2,1)}), bf16[2,16,8,1024]{3,2,0,1:T(8,128)(2,1)}, u32[]{:S(2)}, u32[]{:S(2)}) async-start(bf16[2,16,8,1024]{3,2,0,1:T(8,128)(2,1)} %bitcast.57), calls=%async_computation.3 | async-start | bytes 1048576 | tf_op jit(solution)/shard_map/all_to_all | solution.py:127
  344.8 12.3 %fusion.8.queries_ref = bf16[1024,256]{1,0:T(8,128)(2,1)} fusion(bf16[1024,8192]{1,0:T(8,128)(2,1)} %all-gather.5.cloned.1.call-done, bf16[8192,256]{1,0:T(8,128)(2,1)} %param.34, f32[256]{0:T(256)S(1)} %copy-done.7), kind=kOutput, calls=%fused_computation.17 | convolution fusion | flops 4295491584 | bytes 21496832 | tf_op jit(solution)/shard_map/dot_general | solution.py:113
  357.1 1.9 slice_bitcast_fusion
  358.9 5.0 %causal_attention.1 = bf16[1024,256]{1,0:T(8,128)(2,1)} custom-call(bf16[1024,256]{1,0:T(8,128)(2,1)} %fusion.8.queries_ref, bf16[128,1024]{1,0:T(8,128)(2,1)} %get-tuple-element.6.keys_ref, bf16[128,1024]{1,0:T(8,128)(2,1)} %get-tuple-element.5.values_ref), custom_call_target="tpu_custom_call" | custom-call | tf_op jit(solution)/shard_map/causal_attention/pallas_call | solution.py:172
  (40 shorter events, 1.1 us)
Async XLA Ops:
  6.5 76.9 %copy-start = (bf16[5120,320]{0,1:T(8,128)(2,1)S(1)}, bf16[5120,320]{0,1:T(8,128)(2,1)}, u32[]{:S(2)}) copy-start(bf16[5120,320]{0,1:T(8,128)(2,1)} %param.29) | copy-start | bytes 9830404
  6.5 76.9 %all-gather.3.cloned.1.call-start = ((), (), s32[]{:S(2)}) async-start(), calls=%async_computation.4 | async-start | bytes 5570560 | tf_op jit(solution)/shard_map/all_gather | solution.py:75
  12.9 9.1 %copy-start.3 = (f32[1280]{0:T(1024)S(1)}, f32[1280]{0:T(1024)}, u32[]{:S(2)}) copy-start(f32[1280]{0:T(1024)} %param.28) | copy-start | bytes 15364
  14.9 68.5 %copy-start.6 = (f32[320]{0:T(512)S(1)}, f32[320]{0:T(512)}, u32[]{:S(2)}) copy-start(f32[320]{0:T(512)} %param.30) | copy-start | bytes 3844
  24.8 161.1 %reduce-scatter.2.cloned.1.call-start = ((), (), s32[]{:S(2)}) async-start(), calls=%async_computation.5 | async-start | bytes 8912896 | tf_op jit(solution)/shard_map/reduce_scatter | solution.py:80
  100.1 0.7 copy-start.4
  100.1 85.7 %copy-start.2 = (f32[8192]{0:T(1024)S(1)}, f32[8192]{0:T(1024)}, u32[]{:S(2)}) copy-start(f32[8192]{0:T(1024)} %param.32) | copy-start | bytes 98308
  100.1 93.0 %copy-start.8 = (s32[1,64]{1,0:T(1,128)S(1)}, s32[1,64]{1,0:T(1,128)}, u32[]{:S(2)}) copy-start(s32[1,64]{1,0:T(1,128)} %param.22) | copy-start | bytes 772
  101.9 86.6 %all-to-all-start = ((s32[8,1,8]{2,1,0:T(1,128)}), s32[8,1,8]{2,1,0:T(1,128)S(1)}, u32[]{:S(2)}, u32[]{:S(2)}) async-start(s32[8,1,8]{2,1,0:T(1,128)} %bitcast.1), calls=%async_computation | async-start | bytes 8192 | tf_op jit(solution)/shard_map/all_to_all | solution.py:104
  188.5 20.5 %all-to-all-start.1 = ((bf16[8,8,8192]{2,1,0:T(8,128)(2,1)}), bf16[8,8,8192]{2,1,0:T(8,128)(2,1)}, u32[]{:S(2)}, u32[]{:S(2)}) async-start(bf16[8,8,8192]{2,1,0:T(8,128)(2,1)} %fusion.1), calls=%async_computation.2 | async-start | bytes 2097152 | tf_op jit(solution)/shard_map/all_to_all | solution.py:103
  192.9 134.3 %all-gather.5.cloned.1.call-start = ((), (), s32[]{:S(2)}) async-start(), calls=%async_computation.6 | async-start | bytes 17825792 | tf_op jit(solution)/shard_map/all_gather | solution.py:112
  209.0 6.6 %copy-start.1 = (f32[8192]{0:T(1024)S(1)}, f32[8192]{0:T(1024)}, u32[]{:S(2)}) copy-start(f32[8192]{0:T(1024)} %param.33) | copy-start | bytes 98308
  327.2 11.2 %copy-start.5 = (f32[2,32]{1,0:T(2,128)S(1)}, f32[2,32]{1,0:T(2,128)}, u32[]{:S(2)}) copy-start(f32[2,32]{1,0:T(2,128)} %param.37) | copy-start | bytes 772
  327.2 17.6 %copy-start.7 = (f32[256]{0:T(256)S(1)}, f32[256]{0:T(256)}, u32[]{:S(2)}) copy-start(f32[256]{0:T(256)} %param.35) | copy-start | bytes 3076
  339.5 17.6 %all-to-all-start.2 = ((bf16[2,16,8,1024]{3,2,0,1:T(8,128)(2,1)}), bf16[2,16,8,1024]{3,2,0,1:T(8,128)(2,1)}, u32[]{:S(2)}, u32[]{:S(2)}) async-start(bf16[2,16,8,1024]{3,2,0,1:T(8,128)(2,1)} %bitcast.57), calls=%async_computation.3 | async-start | bytes 1048576 | tf_op jit(solution)/shard_map/all_to_all | solution.py:127
Sparse Core Ops, SparseCore 0:
  24.9 58.5 all-gather.2
  100.3 85.5 reduce-scatter.1
  218.7 108.4 all-gather.4
